TPU v7x, 32 devices: a whole 2x2x4 slice. The times are simulated.
32 devices in a mesh: section: 4 (over y, core), expert: 8 (over z, x).
Axes of the slice: x: 2, y: 2, z: 4, core: 2. Of those that a mesh axis runs over, the one named last changes fastest.
Arguments:
- inputs: bfloat16 [4, 1024, 1024], P('section', 'expert'), may hold values from -6 to 6
- out_grads: bfloat16 [4, 1024, 1024], P('section', 'expert'), may hold values from -6 to 6
- expert_ids: int32 [4, 1024, 8], P('section', 'expert'), may hold values from 0 to 15, all different within a row; in each aligned block of 128 rows (0 to 127, 128 to 255, ..., all dimensions but the last counted through in order) at most 96 rows name the same one
- route_levels: int32 [4, 1024, 8], P('section', 'expert'), may hold values from 8 to 256
- w_gate: bfloat16 [4, 16, 1024, 384], P('section', 'expert'), may hold values from -0.1875 to 0.1875
- w_up: bfloat16 [4, 16, 1024, 384], P('section', 'expert'), may hold values from -0.1875 to 0.1875
- w_down: bfloat16 [4, 16, 384, 1024], P('section', 'expert'), may hold values from -0.3125 to 0.3125
Outputs:
- upstream: bfloat16 [4, 1024, 1024], P('section', 'expert')
- route_grad: bfloat16 [4, 1024, 8], P('section', 'expert')
- gate_update: bfloat16 [4, 16, 1024, 384], P('section', 'expert')
- up_update: bfloat16 [4, 16, 1024, 384], P('section', 'expert')
- down_update: bfloat16 [4, 16, 384, 1024], P('section', 'expert')
Inputs may be any that keep to these rules, and one draw needn't show every extreme that they name: `expert_ids`: each token names 8 different experts; among the 128 tokens of one aligned block no expert is named more than 96 times.
All inputs are finite; a program needn't handle non-finite values.
Results may differ from a plain program's by a relative error of at most 0.0064.
Values may be sent and summed in bfloat16 or wider, within the bound.
A program may use at most 128 MiB of HBM per device.

v0:
```python
import functools
import math

import jax
import jax.numpy as jnp
from jax import lax
from jax.experimental import pallas as pl
from jax.experimental.pallas import tpu as pltpu
from jax.sharding import PartitionSpec as P

MESH = pl.DeviceIdType.MESH
INFO = 128


def kernel(
    lines, rows, sections,
    in_ref, grad_ref, route_ref, wg_ref, wu_ref, wd_ref,
    up_ref, own_route_ref, gate_ref, up_out_ref, down_ref,
    packed, w_in, w_down, hidden_grads, scaled_all, x_out, x_in, z_out, z_in, token,
    load_sem, weight_sem, store_sem,
    az_send, ax_send, a_recv, rx_send, rx_recv, rz_send, rz_recv, y_send, y_recv,
):
    blocks = lines * rows
    tok, width = in_ref.shape
    local, _, hidden = wg_ref.shape
    me = lax.axis_index("expert")
    section = lax.axis_index("section")
    z, x = me // rows, lax.rem(me, rows)

    def paired(d):
        if lines & (lines - 1):
            return lax.rem(z + d, lines)
        bits = lines.bit_length() - 1
        return sum(((z // 2**i + d // 2**i) % 2) * 2**i for i in range(bits))

    def at(dz, dx):
        return paired(dz) * rows + lax.rem(x + dx, rows)

    loads = [
        pltpu.make_async_copy(in_ref, packed.at[me, :, pl.ds(0, width)], load_sem.at[0]),
        pltpu.make_async_copy(grad_ref, packed.at[me, :, pl.ds(width, width)], load_sem.at[1]),
        pltpu.make_async_copy(route_ref, packed.at[me, :, pl.ds(2 * width, INFO)], load_sem.at[2]),
    ]
    weights = []
    for e in range(local):
        weights.append((wg_ref.at[e], w_in.at[:, pl.ds(2 * e * hidden, hidden)]))
        weights.append((wu_ref.at[e], w_in.at[:, pl.ds((2 * e + 1) * hidden, hidden)]))
        weights.append((wd_ref.at[e], w_down.at[pl.ds(e * hidden, hidden), :]))
    weights = [pltpu.make_async_copy(a, b, weight_sem.at[i]) for i, (a, b) in enumerate(weights)]
    for copy in loads + weights:
        copy.start()

    barrier = pltpu.get_barrier_semaphore()
    for dz in range(1, lines):
        pl.semaphore_signal(barrier, inc=1, device_id={"expert": at(dz, 0)}, device_id_type=MESH)
    for dx in range(1, rows):
        pl.semaphore_signal(barrier, inc=1, device_id={"expert": at(0, dx)}, device_id_type=MESH)
    before = lax.rem(section + sections - 1, sections)
    after = lax.rem(section + 1, sections)
    for other in (before, after):
        pl.semaphore_signal(barrier, inc=1, device_id={"section": other}, device_id_type=MESH)
    pl.semaphore_wait(barrier, lines + rows)

    def gather_z(dz):
        return pltpu.make_async_remote_copy(
            src_ref=packed.at[me], dst_ref=packed.at[me],
            send_sem=az_send.at[dz], recv_sem=a_recv.at[me],
            device_id={"expert": at(dz, 0)}, device_id_type=MESH,
        )

    def gather_x(dz, dx):
        block = at(dz, 0)
        return pltpu.make_async_remote_copy(
            src_ref=packed.at[block], dst_ref=packed.at[block],
            send_sem=ax_send.at[dz, dx], recv_sem=a_recv.at[block],
            device_id={"expert": at(0, dx)}, device_id_type=MESH,
        )

    def arrived(block):
        pltpu.make_async_remote_copy(
            src_ref=packed.at[block], dst_ref=packed.at[block],
            send_sem=az_send.at[0], recv_sem=a_recv.at[block],
            device_id={"expert": at(1, 0)}, device_id_type=MESH,
        ).wait_recv()

    def reduce_x(dz, dx):
        line = paired(dz)
        return pltpu.make_async_remote_copy(
            src_ref=x_out.at[line, dx - 1], dst_ref=x_in.at[line, dx - 1],
            send_sem=rx_send.at[line, dx - 1], recv_sem=rx_recv.at[line, dx - 1],
            device_id={"expert": at(0, dx)}, device_id_type=MESH,
        )

    def reduce_z(dz):
        line = paired(dz)
        return pltpu.make_async_remote_copy(
            src_ref=z_out.at[line], dst_ref=z_in.at[dz],
            send_sem=rz_send.at[dz], recv_sem=rz_recv.at[dz],
            device_id={"expert": at(dz, 0)}, device_id_type=MESH,
        )

    for copy in loads:
        copy.wait()
    for dx in range(1, rows):
        gather_x(0, dx).start()
    for dz in range(1, lines):
        gather_z(dz).start()
    for copy in weights:
        copy.wait()

    catalog = lax.broadcasted_iota(jnp.int32, (tok, INFO), 1)
    first = me * local
    last_dims = (((1,), (1,)), ((), ()))

    def compute(block):
        route_all = packed[block, :, pl.ds(2 * width, INFO)].astype(jnp.float32)
        pre = jnp.dot(packed[block, :, pl.ds(0, width)], w_in[...], preferred_element_type=jnp.float32)
        back_all = lax.dot_general(
            packed[block, :, pl.ds(width, width)], w_down[...], last_dims,
            preferred_element_type=jnp.float32,
        )
        route_out = jnp.zeros((tok, INFO), jnp.float32)
        for e in range(local):
            mine = catalog == first + e
            route = jnp.sum(jnp.where(mine, route_all, 0.0), axis=1, keepdims=True)
            gate = pre[:, 2 * e * hidden : (2 * e + 1) * hidden]
            up = pre[:, (2 * e + 1) * hidden : (2 * e + 2) * hidden]
            back = back_all[:, e * hidden : (e + 1) * hidden]
            sig = jax.nn.sigmoid(gate)
            silu = gate * sig
            active = silu * up
            route_grad = jnp.sum(active * back, axis=1, keepdims=True)
            route_out = route_out + jnp.where(mine, route_grad, 0.0)
            back = back * route
            hidden_grads[block, :, pl.ds(2 * e * hidden, hidden)] = (
                back * up * sig * (1.0 + gate * (1.0 - sig))
            ).astype(jnp.bfloat16)
            hidden_grads[block, :, pl.ds((2 * e + 1) * hidden, hidden)] = (back * silu).astype(jnp.bfloat16)
            scaled_all[block, :, pl.ds(e * hidden, hidden)] = (active * route).astype(jnp.bfloat16)
        total = lax.dot_general(
            hidden_grads[block], w_in[...], last_dims, preferred_element_type=jnp.float32
        )
        return total.astype(jnp.bfloat16), route_out.astype(jnp.bfloat16)

    def send_line(dz):
        line = paired(dz)
        for dx in range(1, rows):
            reduce_x(dz, dx).wait_recv()
        value = z_out[line].astype(jnp.float32)
        for dx in range(1, rows):
            value = value + x_in[line, dx - 1].astype(jnp.float32)
        z_out[line] = value.astype(jnp.bfloat16)

    def step(j, carry):
        dz, dx = j // rows, lax.rem(j, rows)
        block = at(dz, dx)
        line = paired(dz)

        @pl.when(j > 0)
        def _():
            arrived(block)

        @pl.when((dx == 0) & (dz > 0))
        def _():
            for other in range(1, rows):
                gather_x(dz, other).start()

        total, route_out = compute(block)

        @pl.when(dx == 0)
        def _():
            z_out[line, :, pl.ds(0, width)] = total
            z_out[line, :, pl.ds(width, INFO)] = route_out

        @pl.when(dx > 0)
        def _():
            x_out[line, dx - 1, :, pl.ds(0, width)] = total
            x_out[line, dx - 1, :, pl.ds(width, INFO)] = route_out
            reduce_x(dz, dx).start()

        @pl.when((dx == 0) & (dz > 1))
        def _():
            send_line(dz - 1)
            reduce_z(dz - 1).start()

        return carry

    lax.fori_loop(0, blocks, step, 0)
    send_line(lines - 1)
    reduce_z(lines - 1).start()

    first_dims = (((0,), (0,)), ((), ()))
    all_rows = blocks * tok
    tile = 256 if width % 256 == 0 and (local * hidden) % 256 == 0 else 128

    @pl.loop(0, width // tile)
    def _(c):
        at_c = pl.ds(pl.multiple_of(c * tile, tile), tile)
        left = packed[:, :, at_c].reshape(all_rows, tile)
        right = hidden_grads[...].reshape(all_rows, 2 * local * hidden)
        w_in[at_c, :] = lax.dot_general(
            left, right, first_dims, preferred_element_type=jnp.float32
        ).astype(jnp.bfloat16)

    stores = []
    for e in range(local):
        stores.append((w_in.at[:, pl.ds(2 * e * hidden, hidden)], gate_ref.at[e]))
        stores.append((w_in.at[:, pl.ds((2 * e + 1) * hidden, hidden)], up_out_ref.at[e]))
    for e in range(local):
        stores.append((w_down.at[pl.ds(e * hidden, hidden), :], down_ref.at[e]))
    stores = [pltpu.make_async_copy(a, b, store_sem.at[i]) for i, (a, b) in enumerate(stores)]
    for copy in stores[: 2 * local]:
        copy.start()

    send_line(0)
    value = z_out[z].astype(jnp.float32)
    for dz in range(1, lines):
        reduce_z(dz).wait_recv()
        value = value + z_in[dz].astype(jnp.float32)
    token[...] = value[:, :width].astype(jnp.bfloat16)
    own_route_ref[...] = value[:, width:].astype(jnp.bfloat16)

    hop = pltpu.make_async_remote_copy(
        src_ref=token, dst_ref=up_ref, send_sem=y_send, recv_sem=y_recv,
        device_id={"section": before}, device_id_type=MESH,
    )

    @pl.when(section > 0)
    def _():
        hop.start()

    @pl.when(section == sections - 1)
    def _():
        up_ref[...] = jnp.zeros_like(up_ref)

    @pl.loop(0, local * hidden // tile)
    def _(c):
        at_c = pl.ds(pl.multiple_of(c * tile, tile), tile)
        left = scaled_all[:, :, at_c].reshape(all_rows, tile)
        right = packed[:, :, pl.ds(width, width)].reshape(all_rows, width)
        w_down[at_c, :] = lax.dot_general(
            left, right, first_dims, preferred_element_type=jnp.float32
        ).astype(jnp.bfloat16)

    for copy in stores[2 * local :]:
        copy.start()
    for dz in range(1, lines):
        gather_z(dz).wait_send()
        reduce_z(dz).wait_send()
    for dz in range(lines):
        for dx in range(1, rows):
            gather_x(dz, dx).wait_send()
            reduce_x(dz, dx).wait_send()

    @pl.when(section > 0)
    def _():
        hop.wait_send()

    @pl.when(section < sections - 1)
    def _():
        hop.wait_recv()

    for copy in stores:
        copy.wait()


def body(rows, inputs, out_grads, expert_ids, route_levels, w_gate, w_up, w_down):
    tok, width = inputs.shape[1:]
    local, _, hidden = w_gate.shape[1:]
    blocks = lax.axis_size("expert")
    sections = lax.axis_size("section")
    lines = blocks // rows
    catalog = jnp.arange(INFO, dtype=jnp.int32)
    chosen = expert_ids[0][:, :, None] == catalog
    levels = jnp.sum(jnp.where(chosen, route_levels[0][:, :, None], 0), axis=1)
    routes = (levels.astype(jnp.float32) / 256.0).astype(jnp.bfloat16)
    bf16 = jnp.bfloat16
    anywhere = pl.BlockSpec(memory_space=pl.ANY)
    inside = pl.BlockSpec(memory_space=pltpu.VMEM)
    dma = pltpu.SemaphoreType.DMA
    side = max(rows - 1, 1)
    upstream, own_routes, gates, ups, downs = pl.pallas_call(
        functools.partial(kernel, lines, rows, sections),
        out_shape=(
            jax.ShapeDtypeStruct((tok, width), bf16),
            jax.ShapeDtypeStruct((tok, INFO), bf16),
            jax.ShapeDtypeStruct(w_gate.shape[1:], bf16),
            jax.ShapeDtypeStruct(w_up.shape[1:], bf16),
            jax.ShapeDtypeStruct(w_down.shape[1:], bf16),
        ),
        in_specs=[anywhere] * 6,
        out_specs=(inside, inside, anywhere, anywhere, anywhere),
        scratch_shapes=[
            pltpu.VMEM((blocks, tok, 2 * width + INFO), bf16),
            pltpu.VMEM((width, 2 * local * hidden), bf16),
            pltpu.VMEM((local * hidden, width), bf16),
            pltpu.VMEM((blocks, tok, 2 * local * hidden), bf16),
            pltpu.VMEM((blocks, tok, local * hidden), bf16),
            pltpu.VMEM((lines, side, tok, width + INFO), bf16),
            pltpu.VMEM((lines, side, tok, width + INFO), bf16),
            pltpu.VMEM((lines, tok, width + INFO), bf16),
            pltpu.VMEM((lines, tok, width + INFO), bf16),
            pltpu.VMEM((tok, width), bf16),
            dma((3,)),
            dma((3 * local,)),
            dma((3 * local,)),
            dma((lines,)),
            dma((lines, rows)),
            dma((blocks,)),
            dma((lines, side)),
            dma((lines, side)),
            dma((lines,)),
            dma((lines,)),
            dma,
            dma,
        ],
        compiler_params=pltpu.CompilerParams(
            collective_id=0, has_side_effects=True, vmem_limit_bytes=66_000_000
        ),
    )(inputs[0], out_grads[0], routes, w_gate[0], w_up[0], w_down[0])
    token_route = jnp.sum(
        jnp.where(chosen, own_routes[:, None, :].astype(jnp.float32), 0.0), axis=2
    ).astype(bf16)
    return (upstream[None], token_route[None], gates[None], ups[None], downs[None])


def solution(mesh):
    blocks = mesh.shape["expert"]
    rows = math.isqrt(max(blocks // 2, 1))
    while blocks % rows:
        rows -= 1
    in_specs = (
        P("section", "expert", None),
        P("section", "expert", None),
        P("section", "expert", None),
        P("section", "expert", None),
        P("section", "expert", None, None),
        P("section", "expert", None, None),
        P("section", "expert", None, None),
    )
    out_specs = (
        P("section", "expert", None),
        P("section", "expert", None),
        P("section", "expert", None, None),
        P("section", "expert", None, None),
        P("section", "expert", None, None),
    )
    return jax.shard_map(
        functools.partial(body, rows), mesh=mesh, in_specs=in_specs, out_specs=out_specs, check_vma=False
    )
```

profile of v0, /device:TPU:1, one launch (start us, length us, event | category | flops | bytes accessed | tf_op | source)
XLA Modules:
  0.0 121.3 jit_solution(10395897615972209978)
XLA Ops:
  0.6 0.8 copy.14
  1.4 0.8 copy.15
  2.2 0.3 select_reduce_fusion.1
  2.6 0.6 multiply_convert_fusion.route_ref
  3.2 108.7 %shard_map.110 = (bf16[128,1024]{1,0:T(8,128)(2,1)}, bf16[128,128]{1,0:T(8,128)(2,1)}, bf16[2,1024,384]{2,1,0:T(8,128)(2,1)}, bf16[2,1024,384]{2,1,0:T(8,128)(2,1)}, bf16[2,384,1024]{2,1,0:T(8,128)(2,1)}) custom-call(bf16[128,1024]{1,0:T(8,128)(2,1)} %bitcast.20, bf16[128,1024]{1,0:T(8,128)(2,1)} %bitcast.21, ...), custom_call_target="tpu_custom_call" | custom-call | tf_op jit(solution)/shard_map/pallas_call | solution.py:282
  111.8 0.8 convert_element_type.25
  112.6 0.4 select_reduce_fusion
  113.0 0.7 copy.16
  113.7 1.7 %copy.21 = bf16[1,128,1024]{2,1,0:T(8,128)(2,1)} copy(bf16[1,128,1024]{2,1,0:T(8,128)(2,1)} %bitcast.22) | data formatting | bytes 524288
  115.3 0.0 copy-start.1
  115.3 2.8 %copy.22 = bf16[1,2,1024,384]{3,2,1,0:T(8,128)(2,1)} copy(bf16[1,2,1024,384]{3,2,1,0:T(8,128)(2,1)} %bitcast.16) | data formatting | bytes 3145728
  118.2 0.0 copy-done.1
  118.2 0.0 copy-start
  118.2 1.1 copy.23
  119.3 0.8 copy-done
  120.1 1.1 copy.24
Async XLA Ops:
  115.3 2.8 %copy-start.1 = (bf16[2,1024,384]{2,1,0:T(8,128)(2,1)S(1)}, bf16[2,1024,384]{2,1,0:T(8,128)(2,1)}, u32[]{:S(2)}) copy-start(bf16[2,1024,384]{2,1,0:T(8,128)(2,1)} %get-tuple-element.13) | copy-start | bytes 4718596
  118.2 2.0 %copy-start = (bf16[2,384,1024]{2,1,0:T(8,128)(2,1)S(1)}, bf16[2,384,1024]{2,1,0:T(8,128)(2,1)}, u32[]{:S(2)}) copy-start(bf16[2,384,1024]{2,1,0:T(8,128)(2,1)} %get-tuple-element.14) | copy-start | bytes 4718596
where the time goes:
time: 122 us; the launch traced here: 121 us
  Pallas kernels  109 us (89%)
  local copies, waits for them, and re-layouts  9.85 us (8%)
  other arithmetic  2.12 us (2%)
    pallas_call x1, Pallas kernels, body(): pl.pallas_call(functools.partial(kernel, lines, rows, sections), out_shap...  109 us
    unnamed x9, local copies, waits for them, and re-layouts  8.28 us

commit v1 on v0

v1 whole, which is shorter than its diff:
```python
import functools
import math

import jax
import jax.numpy as jnp
from jax import lax
from jax.experimental import pallas as pl
from jax.experimental.pallas import tpu as pltpu
from jax.sharding import PartitionSpec as P

MESH = pl.DeviceIdType.MESH


def kernel(
    lines, rows, sections,
    ids_ref, levels_ref, in_ref, grad_ref, wg_ref, wu_ref, wd_ref,
    up_ref, own_route_ref, gate_ref, up_out_ref, down_ref,
    acts, grads, routes, w_in, w_down, hidden_grads, scaled_all,
    part_out, part_in, back_out, back_in, token,
    load_sem, weight_sem, store_sem,
    z_send, x_send, act_recv, grad_recv, route_send, route_recv,
    part_send, part_recv, back_send, back_recv, y_send, y_recv,
):
    blocks = lines * rows
    tok, width = in_ref.shape
    local, _, hidden = wg_ref.shape
    experts = blocks * local
    me = lax.axis_index("expert")
    section = lax.axis_index("section")
    z, x = me // rows, lax.rem(me, rows)

    def at(line, dx):
        return line * rows + lax.rem(x + dx, rows)

    nearest_end = jnp.minimum(z, lines - 1 - z)
    inward = jnp.where(2 * z < lines, 1, -1)

    def line_at(k):
        both = k <= 2 * nearest_end
        far = jnp.where(both, (k + 1) // 2, k - nearest_end)
        sign = jnp.where(both & (lax.rem(k, 2) == 0), -inward, inward)
        return z + far * sign

    loads = [
        pltpu.make_async_copy(in_ref, acts.at[me], load_sem.at[0]),
        pltpu.make_async_copy(grad_ref, grads.at[me], load_sem.at[1]),
    ]
    weights = []
    for e in range(local):
        weights.append((wg_ref.at[e], w_in.at[:, pl.ds(2 * e * hidden, hidden)]))
        weights.append((wu_ref.at[e], w_in.at[:, pl.ds((2 * e + 1) * hidden, hidden)]))
        weights.append((wd_ref.at[e], w_down.at[pl.ds(e * hidden, hidden), :]))
    weights = [pltpu.make_async_copy(a, b, weight_sem.at[i]) for i, (a, b) in enumerate(weights)]
    for copy in loads + weights:
        copy.start()

    barrier = pltpu.get_barrier_semaphore()
    for d in range(1, blocks):
        pl.semaphore_signal(
            barrier, inc=1, device_id={"expert": lax.rem(me + d, blocks)}, device_id_type=MESH
        )
    before = lax.rem(section + sections - 1, sections)
    after = lax.rem(section + 1, sections)
    for other in (before, after):
        pl.semaphore_signal(barrier, inc=1, device_id={"section": other}, device_id_type=MESH)

    ids = ids_ref[...]
    levels = levels_ref[...]
    expert_row = lax.broadcasted_iota(jnp.int32, (experts, tok), 0)
    mine_routes = jnp.zeros((experts, tok), jnp.float32)
    for k in range(ids.shape[0]):
        level = levels[k : k + 1, :].astype(jnp.float32) * (1.0 / 256.0)
        mine_routes = mine_routes + jnp.where(ids[k : k + 1, :] == expert_row, level, 0.0)
    routes[me] = mine_routes

    pl.semaphore_wait(barrier, blocks + 1)

    halves = ((acts, act_recv), (grads, grad_recv))

    def z_copy(line, side, half):
        buffer, recv = halves[half]
        block = at(line, 0)
        return pltpu.make_async_remote_copy(
            src_ref=buffer.at[block], dst_ref=buffer.at[block],
            send_sem=z_send.at[line, (side + 1) // 2, half], recv_sem=recv.at[block],
            device_id={"expert": me + side * rows}, device_id_type=MESH,
        )

    def x_copy(line, dx, half):
        buffer, recv = halves[half]
        block = at(line, 0)
        return pltpu.make_async_remote_copy(
            src_ref=buffer.at[block], dst_ref=buffer.at[block],
            send_sem=x_send.at[line, dx, half], recv_sem=recv.at[block],
            device_id={"expert": at(z, dx)}, device_id_type=MESH,
        )

    def arrived(block, half):
        buffer, recv = halves[half]
        pltpu.make_async_remote_copy(
            src_ref=buffer.at[block], dst_ref=buffer.at[block],
            send_sem=x_send.at[0, 0, half], recv_sem=recv.at[block],
            device_id={"expert": at(z, 1)}, device_id_type=MESH,
        ).wait_recv()

    def passes(line, side):
        if side > 0:
            return (line <= z) & (z < lines - 1)
        return (line >= z) & (z > 0)

    def forward(line, half):
        for side in (1, -1):
            @pl.when(passes(line, side))
            def _():
                z_copy(line, side, half).start()
        for dx in range(1, rows):
            x_copy(line, dx, half).start()

    def route_copy(d):
        other = lax.rem(me + d, blocks)
        return pltpu.make_async_remote_copy(
            src_ref=routes.at[me], dst_ref=routes.at[me],
            send_sem=route_send.at[d], recv_sem=route_recv.at[me],
            device_id={"expert": other}, device_id_type=MESH,
        )

    def part_copy(block):
        return pltpu.make_async_remote_copy(
            src_ref=part_out.at[block], dst_ref=part_in.at[me],
            send_sem=part_send.at[block], recv_sem=part_recv.at[me],
            device_id={"expert": block}, device_id_type=MESH,
        )

    def back_copy(block):
        return pltpu.make_async_remote_copy(
            src_ref=back_out.at[block], dst_ref=back_in.at[me],
            send_sem=back_send.at[block], recv_sem=back_recv.at[me],
            device_id={"expert": block}, device_id_type=MESH,
        )

    for half in range(2):
        loads[half].wait()
        forward(z, half)
    for d in range(1, blocks):
        route_copy(d).start()
    for copy in weights:
        copy.wait()

    last_dims = (((1,), (1,)), ((), ()))
    first = me * local
    diagonal = lax.broadcasted_iota(jnp.int32, (tok, tok), 0) == lax.broadcasted_iota(
        jnp.int32, (tok, tok), 1
    )
    back_row = lax.broadcasted_iota(jnp.int32, back_out.shape[1:], 0)

    def compute(block):
        pre = jnp.dot(acts[block], w_in[...], preferred_element_type=jnp.float32)
        back_all = lax.dot_general(
            grads[block], w_down[...], last_dims, preferred_element_type=jnp.float32
        )
        block_routes = routes[block]
        route_rows = jnp.zeros(back_out.shape[1:], jnp.float32)
        for e in range(local):
            route = jnp.sum(jnp.where(expert_row == first + e, block_routes, 0.0), axis=0, keepdims=True)
            route = jnp.sum(jnp.where(diagonal, route, 0.0), axis=1, keepdims=True)
            gate = pre[:, 2 * e * hidden : (2 * e + 1) * hidden]
            up = pre[:, (2 * e + 1) * hidden : (2 * e + 2) * hidden]
            back = back_all[:, e * hidden : (e + 1) * hidden]
            sig = jax.nn.sigmoid(gate)
            silu = gate * sig
            active = silu * up
            route_grad = jnp.sum(active * back, axis=1, keepdims=True)
            route_grad = jnp.sum(jnp.where(diagonal, route_grad, 0.0), axis=0, keepdims=True)
            route_rows = route_rows + jnp.where(back_row == e, route_grad, 0.0)
            back = back * route
            hidden_grads[block, :, pl.ds(2 * e * hidden, hidden)] = (
                back * up * sig * (1.0 + gate * (1.0 - sig))
            ).astype(jnp.bfloat16)
            hidden_grads[block, :, pl.ds((2 * e + 1) * hidden, hidden)] = (back * silu).astype(jnp.bfloat16)
            scaled_all[block, :, pl.ds(e * hidden, hidden)] = (active * route).astype(jnp.bfloat16)
        total = lax.dot_general(
            hidden_grads[block], w_in[...], last_dims, preferred_element_type=jnp.float32
        )
        part_out[block] = total.astype(jnp.bfloat16)
        back_out[block] = route_rows

    def step(j, carry):
        after_first = j - 1
        group = jnp.where(j == 0, 0, after_first // rows + 1)
        dx = jnp.where(j == 0, 0, lax.rem(after_first + rows, rows) + jnp.where(group == lines, 1, 0))
        line = line_at(group - jnp.where(dx > 0, 1, 0))
        block = at(line, dx)

        @pl.when((dx == 0) & (j > 0))
        def _():
            for half in range(2):
                arrived(block, half)
                forward(line, half)

        @pl.when(dx > 0)
        def _():
            for half in range(2):
                arrived(block, half)

        @pl.when(j > 0)
        def _():
            pltpu.make_async_remote_copy(
                src_ref=routes.at[block], dst_ref=routes.at[block],
                send_sem=route_send.at[0], recv_sem=route_recv.at[block],
                device_id={"expert": at(z, 1)}, device_id_type=MESH,
            ).wait_recv()

        compute(block)

        @pl.when(j > 0)
        def _():
            part_copy(block).start()
            back_copy(block).start()

        return carry

    lax.fori_loop(0, blocks, step, 0)

    first_dims = (((0,), (0,)), ((), ()))
    all_rows = blocks * tok
    tile = 256 if width % 256 == 0 and (local * hidden) % 256 == 0 else 128

    @pl.loop(0, width // tile)
    def _(c):
        at_c = pl.ds(pl.multiple_of(c * tile, tile), tile)
        left = acts[:, :, at_c].reshape(all_rows, tile)
        right = hidden_grads[...].reshape(all_rows, 2 * local * hidden)
        w_in[at_c, :] = lax.dot_general(
            left, right, first_dims, preferred_element_type=jnp.float32
        ).astype(jnp.bfloat16)

    stores = []
    for e in range(local):
        stores.append((w_in.at[:, pl.ds(2 * e * hidden, hidden)], gate_ref.at[e]))
        stores.append((w_in.at[:, pl.ds((2 * e + 1) * hidden, hidden)], up_out_ref.at[e]))
    for e in range(local):
        stores.append((w_down.at[pl.ds(e * hidden, hidden), :], down_ref.at[e]))
    stores = [pltpu.make_async_copy(a, b, store_sem.at[i]) for i, (a, b) in enumerate(stores)]
    for copy in stores[: 2 * local]:
        copy.start()

    @pl.loop(0, local * hidden // tile)
    def _(c):
        at_c = pl.ds(pl.multiple_of(c * tile, tile), tile)
        left = scaled_all[:, :, at_c].reshape(all_rows, tile)
        right = grads[...].reshape(all_rows, width)
        w_down[at_c, :] = lax.dot_general(
            left, right, first_dims, preferred_element_type=jnp.float32
        ).astype(jnp.bfloat16)

    for copy in stores[2 * local :]:
        copy.start()

    value = part_out[me].astype(jnp.float32)
    for d in range(1, blocks):
        other = lax.rem(me + d, blocks)
        pltpu.make_async_remote_copy(
            src_ref=part_out.at[other], dst_ref=part_in.at[other],
            send_sem=part_send.at[other], recv_sem=part_recv.at[other],
            device_id={"expert": other}, device_id_type=MESH,
        ).wait_recv()
        value = value + part_in[other].astype(jnp.float32)
    token[...] = value.astype(jnp.bfloat16)

    hop = pltpu.make_async_remote_copy(
        src_ref=token, dst_ref=up_ref, send_sem=y_send, recv_sem=y_recv,
        device_id={"section": before}, device_id_type=MESH,
    )

    @pl.when(section > 0)
    def _():
        hop.start()

    @pl.when(section == sections - 1)
    def _():
        up_ref[...] = jnp.zeros_like(up_ref)

    back_in[me] = back_out[me]
    for d in range(1, blocks):
        other = lax.rem(me + d, blocks)
        pltpu.make_async_remote_copy(
            src_ref=back_out.at[other], dst_ref=back_in.at[other],
            send_sem=back_send.at[other], recv_sem=back_recv.at[other],
            device_id={"expert": other}, device_id_type=MESH,
        ).wait_recv()
    route_total = jnp.zeros(ids.shape, jnp.float32)
    for b in range(blocks):
        rows_of = back_in[b]
        for e in range(local):
            route_total = route_total + jnp.where(ids == b * local + e, rows_of[e : e + 1, :], 0.0)
    own_route_ref[...] = route_total.astype(jnp.bfloat16)

    for line in range(lines):
        for half in range(2):
            for side in (1, -1):
                @pl.when(passes(line, side))
                def _():
                    z_copy(line, side, half).wait_send()
            for dx in range(1, rows):
                x_copy(line, dx, half).wait_send()
    for d in range(1, blocks):
        other = lax.rem(me + d, blocks)
        route_copy(d).wait_send()
        part_copy(other).wait_send()
        back_copy(other).wait_send()

    @pl.when(section > 0)
    def _():
        hop.wait_send()

    @pl.when(section < sections - 1)
    def _():
        hop.wait_recv()

    for copy in stores:
        copy.wait()


def body(rows, inputs, out_grads, expert_ids, route_levels, w_gate, w_up, w_down):
    tok, width = inputs.shape[1:]
    local, _, hidden = w_gate.shape[1:]
    blocks = lax.axis_size("expert")
    sections = lax.axis_size("section")
    lines = blocks // rows
    experts = blocks * local
    top = expert_ids.shape[2]
    bf16 = jnp.bfloat16
    f32 = jnp.float32
    anywhere = pl.BlockSpec(memory_space=pl.ANY)
    inside = pl.BlockSpec(memory_space=pltpu.VMEM)
    dma = pltpu.SemaphoreType.DMA
    back_rows = -(-local // 8) * 8
    upstream, own_routes, gates, ups, downs = pl.pallas_call(
        functools.partial(kernel, lines, rows, sections),
        out_shape=(
            jax.ShapeDtypeStruct((tok, width), bf16),
            jax.ShapeDtypeStruct((top, tok), bf16),
            jax.ShapeDtypeStruct(w_gate.shape[1:], bf16),
            jax.ShapeDtypeStruct(w_up.shape[1:], bf16),
            jax.ShapeDtypeStruct(w_down.shape[1:], bf16),
        ),
        in_specs=[inside] * 2 + [anywhere] * 5,
        out_specs=(inside, inside, anywhere, anywhere, anywhere),
        scratch_shapes=[
            pltpu.VMEM((blocks, tok, width), bf16),
            pltpu.VMEM((blocks, tok, width), bf16),
            pltpu.VMEM((blocks, experts, tok), f32),
            pltpu.VMEM((width, 2 * local * hidden), bf16),
            pltpu.VMEM((local * hidden, width), bf16),
            pltpu.VMEM((blocks, tok, 2 * local * hidden), bf16),
            pltpu.VMEM((blocks, tok, local * hidden), bf16),
            pltpu.VMEM((blocks, tok, width), bf16),
            pltpu.VMEM((blocks, tok, width), bf16),
            pltpu.VMEM((blocks, back_rows, tok), f32),
            pltpu.VMEM((blocks, back_rows, tok), f32),
            pltpu.VMEM((tok, width), bf16),
            dma((2,)),
            dma((3 * local,)),
            dma((3 * local,)),
            dma((lines, 2, 2)),
            dma((lines, rows, 2)),
            dma((blocks,)),
            dma((blocks,)),
            dma((blocks,)),
            dma((blocks,)),
            dma((blocks,)),
            dma((blocks,)),
            dma((blocks,)),
            dma((blocks,)),
            dma,
            dma,
        ],
        compiler_params=pltpu.CompilerParams(
            collective_id=0, has_side_effects=True, vmem_limit_bytes=66_000_000
        ),
    )(
        jnp.swapaxes(expert_ids[0], 0, 1), jnp.swapaxes(route_levels[0], 0, 1),
        inputs[0], out_grads[0], w_gate[0], w_up[0], w_down[0],
    )
    token_route = jnp.swapaxes(own_routes, 0, 1)
    return (upstream[None], token_route[None], gates[None], ups[None], downs[None])


def solution(mesh):
    blocks = mesh.shape["expert"]
    rows = math.isqrt(max(blocks // 2, 1))
    while blocks % rows:
        rows -= 1
    in_specs = (
        P("section", "expert", None),
        P("section", "expert", None),
        P("section", "expert", None),
        P("section", "expert", None),
        P("section", "expert", None, None),
        P("section", "expert", None, None),
        P("section", "expert", None, None),
    )
    out_specs = (
        P("section", "expert", None),
        P("section", "expert", None),
        P("section", "expert", None, None),
        P("section", "expert", None, None),
        P("section", "expert", None, None),
    )
    return jax.shard_map(
        functools.partial(body, rows), mesh=mesh, in_specs=in_specs, out_specs=out_specs, check_vma=False
    )
```

time: 122 us -> 102 us (0.84)
  Pallas kernels: 109 us -> 92.4 us
  other arithmetic: 2.12 us -> 0 us
    pallas_call x1, Pallas kernels: 109 us -> 92.4 us  [body(): pl.pallas_call(functools.partial(kernel, lines, rows, sections), out_shap...]
    convert_element_type x2 -> x0, other arithmetic: 1.39 us -> none  [the longest x1 0.76 us: body(): own_routes[:, None, :].astype(jnp.float32)]
where the time goes in v1:
time: 102 us
  Pallas kernels  92.4 us (91%)
  local copies, waits for them, and re-layouts  8.87 us (9%)
    pallas_call x1, Pallas kernels, body(): pl.pallas_call(functools.partial(kernel, lines, rows, sections), out_shap...  92.4 us
    unnamed x9, local copies, waits for them, and re-layouts  8.87 us

profile of v1, /device:TPU:1, one launch (start us, length us, event | category | flops | bytes accessed | tf_op | source)
XLA Modules:
  0.0 101.9 jit_solution(3281221904498948822)
XLA Ops:
  0.6 92.4 %shard_map.110 = (bf16[128,1024]{1,0:T(8,128)(2,1)}, bf16[8,128]{1,0:T(8,128)(2,1)}, bf16[2,1024,384]{2,1,0:T(8,128)(2,1)}, bf16[2,1024,384]{2,1,0:T(8,128)(2,1)}, bf16[2,384,1024]{2,1,0:T(8,128)(2,1)}) custom-call(s32[8,128]{1,0:T(8,128)} %bitcast.27, s32[8,128]{1,0:T(8,128)} %bitcast.28, bf16[128,1024]{1,0:T(8,128)(2,1)} %bitcast.24, ...), custom_call_target="tpu_custom_call" | custom-call | tf_op jit(solution)/shard_map/pallas_call | solution.py:338
  93.0 1.7 %copy.17 = bf16[1,128,1024]{2,1,0:T(8,128)(2,1)} copy(bf16[1,128,1024]{2,1,0:T(8,128)(2,1)} %bitcast.26) | data formatting | bytes 524288
  94.7 1.3 %copy.18 = bf16[1,128,8]{1,2,0:T(8,128)(2,1)} copy(bf16[1,128,8]{1,2,0:T(8,128)(2,1)} %bitcast.29) | data formatting | bytes 4096
  96.0 0.0 copy-start.1
  96.0 2.8 %copy.19 = bf16[1,2,1024,384]{3,2,1,0:T(8,128)(2,1)} copy(bf16[1,2,1024,384]{3,2,1,0:T(8,128)(2,1)} %bitcast.20) | data formatting | bytes 3145728
  98.8 0.0 copy-done.1
  98.8 0.0 copy-start
  98.8 1.1 %copy.20 = bf16[1,2,1024,384]{3,2,1,0:T(8,128)(2,1)} copy(bf16[1,2,1024,384]{3,2,1,0:T(8,128)(2,1)S(1)} %bitcast.19) | data formatting | bytes 3145728
  99.9 0.8 copy-done
  100.8 1.1 %copy.21 = bf16[1,2,384,1024]{3,2,1,0:T(8,128)(2,1)} copy(bf16[1,2,384,1024]{3,2,1,0:T(8,128)(2,1)S(1)} %bitcast.18) | data formatting | bytes 3145728
Async XLA Ops:
  96.0 2.8 %copy-start.1 = (bf16[2,1024,384]{2,1,0:T(8,128)(2,1)S(1)}, bf16[2,1024,384]{2,1,0:T(8,128)(2,1)}, u32[]{:S(2)}) copy-start(bf16[2,1024,384]{2,1,0:T(8,128)(2,1)} %get-tuple-element.13) | copy-start | bytes 4718596
  98.8 2.0 %copy-start = (bf16[2,384,1024]{2,1,0:T(8,128)(2,1)S(1)}, bf16[2,384,1024]{2,1,0:T(8,128)(2,1)}, u32[]{:S(2)}) copy-start(bf16[2,384,1024]{2,1,0:T(8,128)(2,1)} %get-tuple-element.14) | copy-start | bytes 4718596

commit v2 on v1

--- a/solution.py
+++ b/solution.py
@@ -9,6 +9,9 @@
 from jax.sharding import PartitionSpec as P
 
 MESH = pl.DeviceIdType.MESH
+COLUMN = (1,)
+STRAIGHT = ()
+CUTS = 2
 
 
 def kernel(
@@ -16,10 +19,10 @@
     ids_ref, levels_ref, in_ref, grad_ref, wg_ref, wu_ref, wd_ref,
     up_ref, own_route_ref, gate_ref, up_out_ref, down_ref,
     acts, grads, routes, w_in, w_down, hidden_grads, scaled_all,
-    part_out, part_in, back_out, back_in, token,
-    load_sem, weight_sem, store_sem,
+    col_out, col_in, side_out, side_in, back_out, back_in, token, total_ref,
+    load_sem, weight_sem,
     z_send, x_send, act_recv, grad_recv, route_send, route_recv,
-    part_send, part_recv, back_send, back_recv, y_send, y_recv,
+    col_send, col_recv, side_send, side_recv, back_send, back_recv, y_send, y_recv,
 ):
     blocks = lines * rows
     tok, width = in_ref.shape
@@ -124,12 +127,51 @@
             device_id={"expert": other}, device_id_type=MESH,
         )
 
-    def part_copy(block):
-        return pltpu.make_async_remote_copy(
-            src_ref=part_out.at[block], dst_ref=part_in.at[me],
-            send_sem=part_send.at[block], recv_sem=part_recv.at[me],
-            device_id={"expert": block}, device_id_type=MESH,
-        )
+    def away(line):
+        return jnp.abs(line - z)
+
+    def among(line, distances):
+        return functools.reduce(jnp.logical_or, [away(line) == d for d in distances], line != line)
+
+    def by_side(line):
+        return (line != z) & ~among(line, COLUMN) & ~among(line, STRAIGHT)
+
+    cut_rows = tok // CUTS
+    cuts = [pl.ds(c * cut_rows, cut_rows) for c in range(CUTS)]
+
+    def col_copy(line, c):
+        return pltpu.make_async_remote_copy(
+            src_ref=col_out.at[line, cuts[c]], dst_ref=col_in.at[z, cuts[c]],
+            send_sem=col_send.at[line, c], recv_sem=col_recv.at[z, c],
+            device_id={"expert": at(line, 0)}, device_id_type=MESH,
+        )
+
+    def side_copy(line, dx, slot, target, c):
+        return pltpu.make_async_remote_copy(
+            src_ref=side_out.at[line, dx - 1, cuts[c]], dst_ref=side_in.at[slot, dx - 1, cuts[c]],
+            send_sem=side_send.at[line, dx - 1, c], recv_sem=side_recv.at[slot, dx - 1, c],
+            device_id={"expert": target}, device_id_type=MESH,
+        )
+
+    def start_col(line):
+        @pl.when((line != z) & ~by_side(line))
+        def _():
+            for c in range(CUTS):
+                col_copy(line, c).start()
+
+    def start_side(line, dx):
+        for c in range(CUTS):
+            @pl.when(by_side(line))
+            def _():
+                side_copy(line, dx, line, at(z, dx), c).start()
+
+            @pl.when(among(line, COLUMN))
+            def _():
+                side_copy(line, dx, z, at(line, 0), c).start()
+
+            @pl.when(among(line, STRAIGHT))
+            def _():
+                side_copy(line, dx, z, at(line, dx), c).start()
 
     def back_copy(block):
         return pltpu.make_async_remote_copy(
@@ -181,8 +223,8 @@
         total = lax.dot_general(
             hidden_grads[block], w_in[...], last_dims, preferred_element_type=jnp.float32
         )
-        part_out[block] = total.astype(jnp.bfloat16)
         back_out[block] = route_rows
+        return total.astype(jnp.bfloat16)
 
     def step(j, carry):
         after_first = j - 1
@@ -197,6 +239,16 @@
                 arrived(block, half)
                 forward(line, half)
 
+        last_forward = (lines - 2) * rows + 1
+
+        @pl.when(j == last_forward)
+        def _():
+            for k in range(1, lines - 1):
+                start_col(line_at(k))
+            for k in range(1, lines - 2):
+                for other in range(1, rows):
+                    start_side(line_at(k), other)
+
         @pl.when(dx > 0)
         def _():
             for half in range(2):
@@ -210,16 +262,58 @@
                 device_id={"expert": at(z, 1)}, device_id_type=MESH,
             ).wait_recv()
 
-        compute(block)
+        total = compute(block)
 
         @pl.when(j > 0)
         def _():
-            part_copy(block).start()
             back_copy(block).start()
 
+        @pl.when(dx == 0)
+        def _():
+            col_out[line] = total
+
+            @pl.when(j >= last_forward)
+            def _():
+                start_col(line)
+
+        @pl.when(dx > 0)
+        def _():
+            side_out[line, dx - 1] = total
+
+            @pl.when(j >= last_forward)
+            def _():
+                start_side(line, dx)
+
         return carry
 
     lax.fori_loop(0, blocks, step, 0)
+
+    def side_arrived(line, dx, c):
+        side_copy(line, dx, line, at(z, 1), c).wait_recv()
+
+    for c in range(CUTS):
+        for k in range(1, lines):
+            line = line_at(k)
+
+            @pl.when(by_side(line))
+            def _():
+                value = col_out[line, cuts[c]].astype(jnp.float32)
+                for dx in range(1, rows):
+                    side_arrived(line, dx, c)
+                    value = value + side_in[line, dx - 1, cuts[c]].astype(jnp.float32)
+                col_out[line, cuts[c]] = value.astype(jnp.bfloat16)
+                col_copy(line, c).start()
+
+        for dx in range(1, rows):
+            for line in range(lines):
+                @pl.when(among(line, COLUMN))
+                def _():
+                    side_arrived(line, dx, c)
+                    side_out[z, dx - 1, cuts[c]] = (
+                        side_out[z, dx - 1, cuts[c]].astype(jnp.float32)
+                        + side_in[line, dx - 1, cuts[c]].astype(jnp.float32)
+                    ).astype(jnp.bfloat16)
+            side_copy(z, dx, z, at(z, dx), c).start()
 
     first_dims = (((0,), (0,)), ((), ()))
     all_rows = blocks * tok
@@ -230,55 +324,62 @@
         at_c = pl.ds(pl.multiple_of(c * tile, tile), tile)
         left = acts[:, :, at_c].reshape(all_rows, tile)
         right = hidden_grads[...].reshape(all_rows, 2 * local * hidden)
-        w_in[at_c, :] = lax.dot_general(
+        update = lax.dot_general(
             left, right, first_dims, preferred_element_type=jnp.float32
         ).astype(jnp.bfloat16)
-
-    stores = []
+        for e in range(local):
+            gate_ref[e, at_c, :] = update[:, 2 * e * hidden : (2 * e + 1) * hidden]
+            up_out_ref[e, at_c, :] = update[:, (2 * e + 1) * hidden : (2 * e + 2) * hidden]
+
+    down_tile = 128
     for e in range(local):
-        stores.append((w_in.at[:, pl.ds(2 * e * hidden, hidden)], gate_ref.at[e]))
-        stores.append((w_in.at[:, pl.ds((2 * e + 1) * hidden, hidden)], up_out_ref.at[e]))
-    for e in range(local):
-        stores.append((w_down.at[pl.ds(e * hidden, hidden), :], down_ref.at[e]))
-    stores = [pltpu.make_async_copy(a, b, store_sem.at[i]) for i, (a, b) in enumerate(stores)]
-    for copy in stores[: 2 * local]:
-        copy.start()
-
-    @pl.loop(0, local * hidden // tile)
-    def _(c):
-        at_c = pl.ds(pl.multiple_of(c * tile, tile), tile)
-        left = scaled_all[:, :, at_c].reshape(all_rows, tile)
-        right = grads[...].reshape(all_rows, width)
-        w_down[at_c, :] = lax.dot_general(
-            left, right, first_dims, preferred_element_type=jnp.float32
-        ).astype(jnp.bfloat16)
-
-    for copy in stores[2 * local :]:
-        copy.start()
-
-    value = part_out[me].astype(jnp.float32)
-    for d in range(1, blocks):
-        other = lax.rem(me + d, blocks)
-        pltpu.make_async_remote_copy(
-            src_ref=part_out.at[other], dst_ref=part_in.at[other],
-            send_sem=part_send.at[other], recv_sem=part_recv.at[other],
-            device_id={"expert": other}, device_id_type=MESH,
-        ).wait_recv()
-        value = value + part_in[other].astype(jnp.float32)
-    token[...] = value.astype(jnp.bfloat16)
-
-    hop = pltpu.make_async_remote_copy(
-        src_ref=token, dst_ref=up_ref, send_sem=y_send, recv_sem=y_recv,
-        device_id={"section": before}, device_id_type=MESH,
-    )
-
-    @pl.when(section > 0)
-    def _():
-        hop.start()
+        @pl.loop(0, hidden // down_tile)
+        def _(c):
+            at_left = pl.ds(pl.multiple_of(e * hidden + c * down_tile, down_tile), down_tile)
+            at_c = pl.ds(pl.multiple_of(c * down_tile, down_tile), down_tile)
+            left = scaled_all[:, :, at_left].reshape(all_rows, down_tile)
+            right = grads[...].reshape(all_rows, width)
+            down_ref[e, at_c, :] = lax.dot_general(
+                left, right, first_dims, preferred_element_type=jnp.float32
+            ).astype(jnp.bfloat16)
+
+    def hop(c):
+        return pltpu.make_async_remote_copy(
+            src_ref=token.at[cuts[c]], dst_ref=up_ref.at[cuts[c]], send_sem=y_send.at[c], recv_sem=y_recv.at[c],
+            device_id={"section": before}, device_id_type=MESH,
+        )
 
     @pl.when(section == sections - 1)
     def _():
         up_ref[...] = jnp.zeros_like(up_ref)
+
+    for c in range(CUTS):
+        total_ref[...] = col_out[z, cuts[c]].astype(jnp.float32)
+
+        def take(piece):
+            total_ref[...] = total_ref[...] + piece.astype(jnp.float32)
+
+        for line in range(lines):
+            @pl.when(line != z)
+            def _():
+                pltpu.make_async_remote_copy(
+                    src_ref=col_out.at[line, cuts[c]], dst_ref=col_in.at[line, cuts[c]],
+                    send_sem=col_send.at[line, c], recv_sem=col_recv.at[line, c],
+                    device_id={"expert": at(line, 0)}, device_id_type=MESH,
+                ).wait_recv()
+                take(col_in[line, cuts[c]])
+
+            @pl.when((line == z) | among(line, STRAIGHT))
+            def _():
+                for dx in range(1, rows):
+                    side_arrived(line, dx, c)
+                    take(side_in[line, dx - 1, cuts[c]])
+
+        token[cuts[c], :] = total_ref[...].astype(jnp.bfloat16)
+
+        @pl.when(section > 0)
+        def _():
+            hop(c).start()
 
     back_in[me] = back_out[me]
     for d in range(1, blocks):
@@ -306,18 +407,33 @@
     for d in range(1, blocks):
         other = lax.rem(me + d, blocks)
         route_copy(d).wait_send()
-        part_copy(other).wait_send()
         back_copy(other).wait_send()
-
-    @pl.when(section > 0)
-    def _():
-        hop.wait_send()
-
-    @pl.when(section < sections - 1)
-    def _():
-        hop.wait_recv()
-
-    for copy in stores:
+    for line in range(lines):
+        @pl.when(line != z)
+        def _():
+            for c in range(CUTS):
+                col_copy(line, c).wait_send()
+
+        for dx in range(1, rows):
+            for c in range(CUTS):
+                side_copy(line, dx, z, at(z, dx), c).wait_send()
+
+    for c in range(CUTS):
+        @pl.when(section > 0)
+        def _():
+            hop(c).wait_send()
+
+        @pl.when(section < sections - 1)
+        def _():
+            hop(c).wait_recv()
+
+
+def finish(*refs):
+    sources, targets, sem = refs[:5], refs[5:10], refs[10]
+    copies = [pltpu.make_async_copy(a, b, sem.at[i]) for i, (a, b) in enumerate(zip(sources, targets))]
+    for copy in copies:
+        copy.start()
+    for copy in copies:
         copy.wait()
 
 
@@ -334,18 +450,15 @@
     anywhere = pl.BlockSpec(memory_space=pl.ANY)
     inside = pl.BlockSpec(memory_space=pltpu.VMEM)
     dma = pltpu.SemaphoreType.DMA
+    side = max(rows - 1, 1)
     back_rows = -(-local // 8) * 8
-    upstream, own_routes, gates, ups, downs = pl.pallas_call(
+    shapes = ((tok, width), (top, tok), w_gate.shape[1:], w_up.shape[1:], w_down.shape[1:])
+    limit = 66_900_000 - 2 * sum(-(-math.prod(shape) // 4096) * 4096 for shape in shapes)
+    results = pl.pallas_call(
         functools.partial(kernel, lines, rows, sections),
-        out_shape=(
-            jax.ShapeDtypeStruct((tok, width), bf16),
-            jax.ShapeDtypeStruct((top, tok), bf16),
-            jax.ShapeDtypeStruct(w_gate.shape[1:], bf16),
-            jax.ShapeDtypeStruct(w_up.shape[1:], bf16),
-            jax.ShapeDtypeStruct(w_down.shape[1:], bf16),
-        ),
+        out_shape=tuple(pltpu.VMEM(shape, bf16) for shape in shapes),
         in_specs=[inside] * 2 + [anywhere] * 5,
-        out_specs=(inside, inside, anywhere, anywhere, anywhere),
+        out_specs=(inside,) * 5,
         scratch_shapes=[
             pltpu.VMEM((blocks, tok, width), bf16),
             pltpu.VMEM((blocks, tok, width), bf16),
@@ -354,13 +467,15 @@
             pltpu.VMEM((local * hidden, width), bf16),
             pltpu.VMEM((blocks, tok, 2 * local * hidden), bf16),
             pltpu.VMEM((blocks, tok, local * hidden), bf16),
-            pltpu.VMEM((blocks, tok, width), bf16),
-            pltpu.VMEM((blocks, tok, width), bf16),
+            pltpu.VMEM((lines, tok, width), bf16),
+            pltpu.VMEM((lines, tok, width), bf16),
+            pltpu.VMEM((lines, side, tok, width), bf16),
+            pltpu.VMEM((lines, side, tok, width), bf16),
             pltpu.VMEM((blocks, back_rows, tok), f32),
             pltpu.VMEM((blocks, back_rows, tok), f32),
             pltpu.VMEM((tok, width), bf16),
+            pltpu.VMEM((tok // CUTS, width), f32),
             dma((2,)),
-            dma((3 * local,)),
             dma((3 * local,)),
             dma((lines, 2, 2)),
             dma((lines, rows, 2)),
@@ -368,20 +483,30 @@
             dma((blocks,)),
             dma((blocks,)),
             dma((blocks,)),
+            dma((lines, CUTS)),
+            dma((lines, CUTS)),
+            dma((lines, side, CUTS)),
+            dma((lines, side, CUTS)),
             dma((blocks,)),
             dma((blocks,)),
-            dma((blocks,)),
-            dma((blocks,)),
-            dma,
-            dma,
+            dma((CUTS,)),
+            dma((CUTS,)),
         ],
         compiler_params=pltpu.CompilerParams(
-            collective_id=0, has_side_effects=True, vmem_limit_bytes=66_000_000
+            collective_id=0, has_side_effects=True, vmem_limit_bytes=limit
         ),
     )(
         jnp.swapaxes(expert_ids[0], 0, 1), jnp.swapaxes(route_levels[0], 0, 1),
         inputs[0], out_grads[0], w_gate[0], w_up[0], w_down[0],
     )
+    upstream, own_routes, gates, ups, downs = pl.pallas_call(
+        finish,
+        out_shape=tuple(jax.ShapeDtypeStruct(shape, bf16) for shape in shapes),
+        in_specs=[inside] * 5,
+        out_specs=(anywhere,) * 5,
+        scratch_shapes=[dma((5,))],
+        compiler_params=pltpu.CompilerParams(vmem_limit_bytes=1_000_000),
+    )(*[pltpu.with_memory_space_constraint(r, pltpu.VMEM) for r in results])
     token_route = jnp.swapaxes(own_routes, 0, 1)
     return (upstream[None], token_route[None], gates[None], ups[None], downs[None])
 

time: 102 us -> 84.3 us (0.83)
  Pallas kernels: 92.4 us -> 83.5 us
  local copies, waits for them, and re-layouts: 8.87 us -> 0 us
    pallas_call x1, Pallas kernels: 92.4 us -> 81.2 us  [body(): pl.pallas_call(functools.partial(kernel, lines, rows, sections), out_shap...]
    unnamed x9 -> x0, local copies, waits for them, and re-layouts: 8.87 us -> none
    pallas_call x0 -> x1, Pallas kernels: none -> 2.32 us  [body(): pl.pallas_call(finish, out_shape=tuple((jax.ShapeDtypeStruct(shape, bf16)...]
where the time goes in v2:
time: 84.3 us; the launch traced here: 84.1 us
  Pallas kernels  83.5 us (99%)
    pallas_call x1, Pallas kernels, body(): pl.pallas_call(functools.partial(kernel, lines, rows, sections), out_shap...  81.2 us
    pallas_call x1, Pallas kernels, body(): pl.pallas_call(finish, out_shape=tuple((jax.ShapeDtypeStruct(shape, bf16)...  2.32 us

profile of v2, /device:TPU:1, one launch (start us, length us, event | category | flops | bytes accessed | tf_op | source)
XLA Modules:
  0.0 84.1 jit_solution(9786180154292638049)
XLA Ops:
  0.6 81.2 %shard_map.110 = (bf16[128,1024]{1,0:T(8,128)(2,1)S(1)}, bf16[8,128]{1,0:T(8,128)(2,1)S(1)}, bf16[2,1024,384]{2,1,0:T(8,128)(2,1)S(1)}, bf16[2,1024,384]{2,1,0:T(8,128)(2,1)S(1)}, bf16[2,384,1024]{2,1,0:T(8,128)(2,1)S(1)}) custom-call(s32[8,128]{1,0:T(8,128)} %bitcast.23, s32[8,128]{1,0:T(8,128)} %bitcast.24, bf16[128,1024]{1,0:T(8,128)(2,1)} %bitcast.21, ...), custom_call_target="tpu_custom_call" | custom-call | tf_op jit(solution)/shard_map/pallas_call | solution.py:457
  81.8 2.3 %shard_map.111 = (bf16[128,1024]{1,0:T(8,128)(2,1)}, bf16[8,128]{1,0:T(8,128)(2,1)}, bf16[2,1024,384]{2,1,0:T(8,128)(2,1)}, bf16[2,1024,384]{2,1,0:T(8,128)(2,1)}, bf16[2,384,1024]{2,1,0:T(8,128)(2,1)}) custom-call(bf16[128,1024]{1,0:T(8,128)(2,1)S(1)} %get-tuple-element.15.refs_0_, bf16[8,128]{1,0:T(8,128)(2,1)S(1)} %get-tuple-element.16.refs_1_, ...), custom_call_target="tpu_custom_call" | custom-call | tf_op jit(solution)/shard_map/pallas_call | solution.py:502

commit v3 on v2

--- a/solution.py
+++ b/solution.py
@@ -9,9 +9,8 @@
 from jax.sharding import PartitionSpec as P
 
 MESH = pl.DeviceIdType.MESH
-COLUMN = (1,)
-STRAIGHT = ()
-CUTS = 2
+COLUMN = ((1,), (1,))
+CUTS = len(COLUMN)
 
 
 def kernel(
@@ -19,10 +18,10 @@
     ids_ref, levels_ref, in_ref, grad_ref, wg_ref, wu_ref, wd_ref,
     up_ref, own_route_ref, gate_ref, up_out_ref, down_ref,
     acts, grads, routes, w_in, w_down, hidden_grads, scaled_all,
-    col_out, col_in, side_out, side_in, back_out, back_in, token, total_ref,
-    load_sem, weight_sem,
+    col_out, col_in, side_out, side_in, back_out, back_in, ids_in, levels_in,
+    small_sem, load_sem, weight_sem,
     z_send, x_send, act_recv, grad_recv, route_send, route_recv,
-    col_send, col_recv, side_send, side_recv, back_send, back_recv, y_send, y_recv,
+    col_send, col_recv, side_send, side_recv, back_send, back_recv,
 ):
     blocks = lines * rows
     tok, width = in_ref.shape
@@ -44,6 +43,12 @@
         sign = jnp.where(both & (lax.rem(k, 2) == 0), -inward, inward)
         return z + far * sign
 
+    small = [
+        pltpu.make_async_copy(ids_ref, ids_in, small_sem.at[0]),
+        pltpu.make_async_copy(levels_ref, levels_in, small_sem.at[1]),
+    ]
+    for copy in small:
+        copy.start()
     loads = [
         pltpu.make_async_copy(in_ref, acts.at[me], load_sem.at[0]),
         pltpu.make_async_copy(grad_ref, grads.at[me], load_sem.at[1]),
@@ -64,11 +69,17 @@
         )
     before = lax.rem(section + sections - 1, sections)
     after = lax.rem(section + 1, sections)
-    for other in (before, after):
-        pl.semaphore_signal(barrier, inc=1, device_id={"section": other}, device_id_type=MESH)
-
-    ids = ids_ref[...]
-    levels = levels_ref[...]
+    for dz in range(lines):
+        line = lax.rem(z + dz, lines)
+        for dx in range(rows if dz == 0 else 1):
+            pl.semaphore_signal(
+                barrier, inc=1, device_id={"expert": at(line, dx), "section": after}, device_id_type=MESH
+            )
+
+    for copy in small:
+        copy.wait()
+    ids = ids_in[...]
+    levels = levels_in[...]
     expert_row = lax.broadcasted_iota(jnp.int32, (experts, tok), 0)
     mine_routes = jnp.zeros((experts, tok), jnp.float32)
     for k in range(ids.shape[0]):
@@ -76,7 +87,7 @@
         mine_routes = mine_routes + jnp.where(ids[k : k + 1, :] == expert_row, level, 0.0)
     routes[me] = mine_routes
 
-    pl.semaphore_wait(barrier, blocks + 1)
+    pl.semaphore_wait(barrier, blocks - 1 + lines + rows - 1)
 
     halves = ((acts, act_recv), (grads, grad_recv))
 
@@ -133,8 +144,8 @@
     def among(line, distances):
         return functools.reduce(jnp.logical_or, [away(line) == d for d in distances], line != line)
 
-    def by_side(line):
-        return (line != z) & ~among(line, COLUMN) & ~among(line, STRAIGHT)
+    def by_side(line, c):
+        return (line != z) & ~among(line, COLUMN[c])
 
     cut_rows = tok // CUTS
     cuts = [pl.ds(c * cut_rows, cut_rows) for c in range(CUTS)]
@@ -143,35 +154,32 @@
         return pltpu.make_async_remote_copy(
             src_ref=col_out.at[line, cuts[c]], dst_ref=col_in.at[z, cuts[c]],
             send_sem=col_send.at[line, c], recv_sem=col_recv.at[z, c],
-            device_id={"expert": at(line, 0)}, device_id_type=MESH,
-        )
-
-    def side_copy(line, dx, slot, target, c):
+            device_id={"expert": at(line, 0), "section": before}, device_id_type=MESH,
+        )
+
+    def side_copy(line, dx, slot, target, c, home=None):
         return pltpu.make_async_remote_copy(
             src_ref=side_out.at[line, dx - 1, cuts[c]], dst_ref=side_in.at[slot, dx - 1, cuts[c]],
             send_sem=side_send.at[line, dx - 1, c], recv_sem=side_recv.at[slot, dx - 1, c],
-            device_id={"expert": target}, device_id_type=MESH,
+            device_id={"expert": target, "section": section if home is None else home},
+            device_id_type=MESH,
         )
 
     def start_col(line):
-        @pl.when((line != z) & ~by_side(line))
-        def _():
-            for c in range(CUTS):
+        for c in range(CUTS):
+            @pl.when(~by_side(line, c))
+            def _():
                 col_copy(line, c).start()
 
     def start_side(line, dx):
         for c in range(CUTS):
-            @pl.when(by_side(line))
+            @pl.when(by_side(line, c))
             def _():
                 side_copy(line, dx, line, at(z, dx), c).start()
 
-            @pl.when(among(line, COLUMN))
+            @pl.when(among(line, COLUMN[c]))
             def _():
                 side_copy(line, dx, z, at(line, 0), c).start()
-
-            @pl.when(among(line, STRAIGHT))
-            def _():
-                side_copy(line, dx, z, at(line, dx), c).start()
 
     def back_copy(block):
         return pltpu.make_async_remote_copy(
@@ -243,7 +251,7 @@
 
         @pl.when(j == last_forward)
         def _():
-            for k in range(1, lines - 1):
+            for k in range(lines - 1):
                 start_col(line_at(k))
             for k in range(1, lines - 2):
                 for other in range(1, rows):
@@ -295,7 +303,7 @@
         for k in range(1, lines):
             line = line_at(k)
 
-            @pl.when(by_side(line))
+            @pl.when(by_side(line, c))
             def _():
                 value = col_out[line, cuts[c]].astype(jnp.float32)
                 for dx in range(1, rows):
@@ -306,14 +314,14 @@
 
         for dx in range(1, rows):
             for line in range(lines):
-                @pl.when(among(line, COLUMN))
+                @pl.when(among(line, COLUMN[c]))
                 def _():
                     side_arrived(line, dx, c)
                     side_out[z, dx - 1, cuts[c]] = (
                         side_out[z, dx - 1, cuts[c]].astype(jnp.float32)
                         + side_in[line, dx - 1, cuts[c]].astype(jnp.float32)
                     ).astype(jnp.bfloat16)
-            side_copy(z, dx, z, at(z, dx), c).start()
+            side_copy(z, dx, z, at(z, dx), c, before).start()
 
     first_dims = (((0,), (0,)), ((), ()))
     all_rows = blocks * tok
@@ -343,43 +351,20 @@
                 left, right, first_dims, preferred_element_type=jnp.float32
             ).astype(jnp.bfloat16)
 
-    def hop(c):
-        return pltpu.make_async_remote_copy(
-            src_ref=token.at[cuts[c]], dst_ref=up_ref.at[cuts[c]], send_sem=y_send.at[c], recv_sem=y_recv.at[c],
-            device_id={"section": before}, device_id_type=MESH,
-        )
-
-    @pl.when(section == sections - 1)
-    def _():
-        up_ref[...] = jnp.zeros_like(up_ref)
-
     for c in range(CUTS):
-        total_ref[...] = col_out[z, cuts[c]].astype(jnp.float32)
-
-        def take(piece):
-            total_ref[...] = total_ref[...] + piece.astype(jnp.float32)
-
-        for line in range(lines):
-            @pl.when(line != z)
-            def _():
-                pltpu.make_async_remote_copy(
-                    src_ref=col_out.at[line, cuts[c]], dst_ref=col_in.at[line, cuts[c]],
-                    send_sem=col_send.at[line, c], recv_sem=col_recv.at[line, c],
-                    device_id={"expert": at(line, 0)}, device_id_type=MESH,
-                ).wait_recv()
-                take(col_in[line, cuts[c]])
-
-            @pl.when((line == z) | among(line, STRAIGHT))
-            def _():
-                for dx in range(1, rows):
-                    side_arrived(line, dx, c)
-                    take(side_in[line, dx - 1, cuts[c]])
-
-        token[cuts[c], :] = total_ref[...].astype(jnp.bfloat16)
-
-        @pl.when(section > 0)
-        def _():
-            hop(c).start()
+        value = jnp.zeros((cut_rows, width), jnp.float32)
+        for dx in range(1, rows):
+            side_arrived(z, dx, c)
+            value = value + side_in[z, dx - 1, cuts[c]].astype(jnp.float32)
+        for dz in range(lines):
+            line = lax.rem(z + dz, lines)
+            pltpu.make_async_remote_copy(
+                src_ref=col_out.at[line, cuts[c]], dst_ref=col_in.at[line, cuts[c]],
+                send_sem=col_send.at[line, c], recv_sem=col_recv.at[line, c],
+                device_id={"expert": at(line, 0), "section": before}, device_id_type=MESH,
+            ).wait_recv()
+            value = value + col_in[line, cuts[c]].astype(jnp.float32)
+        up_ref[cuts[c], :] = jnp.where(section == sections - 1, 0.0, value).astype(jnp.bfloat16)
 
     back_in[me] = back_out[me]
     for d in range(1, blocks):
@@ -409,23 +394,12 @@
         route_copy(d).wait_send()
         back_copy(other).wait_send()
     for line in range(lines):
-        @pl.when(line != z)
-        def _():
-            for c in range(CUTS):
-                col_copy(line, c).wait_send()
+        for c in range(CUTS):
+            col_copy(line, c).wait_send()
 
         for dx in range(1, rows):
             for c in range(CUTS):
                 side_copy(line, dx, z, at(z, dx), c).wait_send()
-
-    for c in range(CUTS):
-        @pl.when(section > 0)
-        def _():
-            hop(c).wait_send()
-
-        @pl.when(section < sections - 1)
-        def _():
-            hop(c).wait_recv()
 
 
 def finish(*refs):
@@ -457,7 +431,7 @@
     results = pl.pallas_call(
         functools.partial(kernel, lines, rows, sections),
         out_shape=tuple(pltpu.VMEM(shape, bf16) for shape in shapes),
-        in_specs=[inside] * 2 + [anywhere] * 5,
+        in_specs=[anywhere] * 7,
         out_specs=(inside,) * 5,
         scratch_shapes=[
             pltpu.VMEM((blocks, tok, width), bf16),
@@ -473,8 +447,9 @@
             pltpu.VMEM((lines, side, tok, width), bf16),
             pltpu.VMEM((blocks, back_rows, tok), f32),
             pltpu.VMEM((blocks, back_rows, tok), f32),
-            pltpu.VMEM((tok, width), bf16),
-            pltpu.VMEM((tok // CUTS, width), f32),
+            pltpu.VMEM((top, tok), jnp.int32),
+            pltpu.VMEM((top, tok), jnp.int32),
+            dma((2,)),
             dma((2,)),
             dma((3 * local,)),
             dma((lines, 2, 2)),
@@ -489,8 +464,6 @@
             dma((lines, side, CUTS)),
             dma((blocks,)),
             dma((blocks,)),
-            dma((CUTS,)),
-            dma((CUTS,)),
         ],
         compiler_params=pltpu.CompilerParams(
             collective_id=0, has_side_effects=True, vmem_limit_bytes=limit

time: 84.3 us -> 80.5 us (0.955)
  Pallas kernels: 83.5 us -> 79.7 us
    pallas_call x1, Pallas kernels: 81.2 us -> 77.4 us  [body(): pl.pallas_call(functools.partial(kernel, lines, rows, sections), out_shap...]
where the time goes in v3:
time: 80.5 us; the launch traced here: 80.4 us
  Pallas kernels  79.7 us (99%)
    pallas_call x1, Pallas kernels, body(): pl.pallas_call(functools.partial(kernel, lines, rows, sections), out_shap...  77.4 us
    pallas_call x1, Pallas kernels, body(): pl.pallas_call(finish, out_shape=tuple((jax.ShapeDtypeStruct(shape, bf16)...  2.32 us

profile of v3, /device:TPU:1, one launch (start us, length us, event | category | flops | bytes accessed | tf_op | source)
XLA Modules:
  0.0 80.4 jit_solution(1005036725286289417)
XLA Ops:
  0.6 77.4 %shard_map.110 = (bf16[128,1024]{1,0:T(8,128)(2,1)S(1)}, bf16[8,128]{1,0:T(8,128)(2,1)S(1)}, bf16[2,1024,384]{2,1,0:T(8,128)(2,1)S(1)}, bf16[2,1024,384]{2,1,0:T(8,128)(2,1)S(1)}, bf16[2,384,1024]{2,1,0:T(8,128)(2,1)S(1)}) custom-call(s32[8,128]{1,0:T(8,128)} %bitcast.23, s32[8,128]{1,0:T(8,128)} %bitcast.24, bf16[128,1024]{1,0:T(8,128)(2,1)} %bitcast.21, ...), custom_call_target="tpu_custom_call" | custom-call | tf_op jit(solution)/shard_map/pallas_call | solution.py:431
  78.1 2.3 %shard_map.111 = (bf16[128,1024]{1,0:T(8,128)(2,1)}, bf16[8,128]{1,0:T(8,128)(2,1)}, bf16[2,1024,384]{2,1,0:T(8,128)(2,1)}, bf16[2,1024,384]{2,1,0:T(8,128)(2,1)}, bf16[2,384,1024]{2,1,0:T(8,128)(2,1)}) custom-call(bf16[128,1024]{1,0:T(8,128)(2,1)S(1)} %get-tuple-element.15.refs_0_, bf16[8,128]{1,0:T(8,128)(2,1)S(1)} %get-tuple-element.16.refs_1_, ...), custom_call_target="tpu_custom_call" | custom-call | tf_op jit(solution)/shard_map/pallas_call | solution.py:475

commit v4 on v3

--- a/solution.py
+++ b/solution.py
@@ -203,8 +203,16 @@
     )
     back_row = lax.broadcasted_iota(jnp.int32, back_out.shape[1:], 0)
 
-    def compute(block):
+    def compute(block, wait_grads):
         pre = jnp.dot(acts[block], w_in[...], preferred_element_type=jnp.float32)
+        forward_parts = []
+        for e in range(local):
+            gate = pre[:, 2 * e * hidden : (2 * e + 1) * hidden]
+            up = pre[:, (2 * e + 1) * hidden : (2 * e + 2) * hidden]
+            sig = jax.nn.sigmoid(gate)
+            silu = gate * sig
+            forward_parts.append((silu, silu * up, up * sig * (1.0 + gate * (1.0 - sig))))
+        wait_grads()
         back_all = lax.dot_general(
             grads[block], w_down[...], last_dims, preferred_element_type=jnp.float32
         )
@@ -213,18 +221,14 @@
         for e in range(local):
             route = jnp.sum(jnp.where(expert_row == first + e, block_routes, 0.0), axis=0, keepdims=True)
             route = jnp.sum(jnp.where(diagonal, route, 0.0), axis=1, keepdims=True)
-            gate = pre[:, 2 * e * hidden : (2 * e + 1) * hidden]
-            up = pre[:, (2 * e + 1) * hidden : (2 * e + 2) * hidden]
+            silu, active, slope = forward_parts[e]
             back = back_all[:, e * hidden : (e + 1) * hidden]
-            sig = jax.nn.sigmoid(gate)
-            silu = gate * sig
-            active = silu * up
             route_grad = jnp.sum(active * back, axis=1, keepdims=True)
             route_grad = jnp.sum(jnp.where(diagonal, route_grad, 0.0), axis=0, keepdims=True)
             route_rows = route_rows + jnp.where(back_row == e, route_grad, 0.0)
             back = back * route
             hidden_grads[block, :, pl.ds(2 * e * hidden, hidden)] = (
-                back * up * sig * (1.0 + gate * (1.0 - sig))
+                back * slope
             ).astype(jnp.bfloat16)
             hidden_grads[block, :, pl.ds((2 * e + 1) * hidden, hidden)] = (back * silu).astype(jnp.bfloat16)
             scaled_all[block, :, pl.ds(e * hidden, hidden)] = (active * route).astype(jnp.bfloat16)
@@ -241,26 +245,29 @@
         line = line_at(group - jnp.where(dx > 0, 1, 0))
         block = at(line, dx)
 
-        @pl.when((dx == 0) & (j > 0))
-        def _():
-            for half in range(2):
+        def receive(half):
+            @pl.when(j > 0)
+            def _():
                 arrived(block, half)
+
+            @pl.when((dx == 0) & (j > 0))
+            def _():
                 forward(line, half)
 
+        receive(0)
+
         last_forward = (lines - 2) * rows + 1
 
-        @pl.when(j == last_forward)
-        def _():
-            for k in range(lines - 1):
-                start_col(line_at(k))
-            for k in range(1, lines - 2):
-                for other in range(1, rows):
-                    start_side(line_at(k), other)
-
-        @pl.when(dx > 0)
-        def _():
-            for half in range(2):
-                arrived(block, half)
+        def wait_grads():
+            receive(1)
+
+            @pl.when(j == last_forward)
+            def _():
+                for k in range(lines - 1):
+                    start_col(line_at(k))
+                for k in range(1, lines - 2):
+                    for other in range(1, rows):
+                        start_side(line_at(k), other)
 
         @pl.when(j > 0)
         def _():
@@ -270,7 +277,7 @@
                 device_id={"expert": at(z, 1)}, device_id_type=MESH,
             ).wait_recv()
 
-        total = compute(block)
+        total = compute(block, wait_grads)
 
         @pl.when(j > 0)
         def _():
@@ -350,6 +357,21 @@
             down_ref[e, at_c, :] = lax.dot_general(
                 left, right, first_dims, preferred_element_type=jnp.float32
             ).astype(jnp.bfloat16)
+
+    back_in[me] = back_out[me]
+    for d in range(1, blocks):
+        other = lax.rem(me + d, blocks)
+        pltpu.make_async_remote_copy(
+            src_ref=back_out.at[other], dst_ref=back_in.at[other],
+            send_sem=back_send.at[other], recv_sem=back_recv.at[other],
+            device_id={"expert": other}, device_id_type=MESH,
+        ).wait_recv()
+    route_total = jnp.zeros(ids.shape, jnp.float32)
+    for b in range(blocks):
+        rows_of = back_in[b]
+        for e in range(local):
+            route_total = route_total + jnp.where(ids == b * local + e, rows_of[e : e + 1, :], 0.0)
+    own_route_ref[...] = route_total.astype(jnp.bfloat16)
 
     for c in range(CUTS):
         value = jnp.zeros((cut_rows, width), jnp.float32)
@@ -365,21 +387,6 @@
             ).wait_recv()
             value = value + col_in[line, cuts[c]].astype(jnp.float32)
         up_ref[cuts[c], :] = jnp.where(section == sections - 1, 0.0, value).astype(jnp.bfloat16)
-
-    back_in[me] = back_out[me]
-    for d in range(1, blocks):
-        other = lax.rem(me + d, blocks)
-        pltpu.make_async_remote_copy(
-            src_ref=back_out.at[other], dst_ref=back_in.at[other],
-            send_sem=back_send.at[other], recv_sem=back_recv.at[other],
-            device_id={"expert": other}, device_id_type=MESH,
-        ).wait_recv()
-    route_total = jnp.zeros(ids.shape, jnp.float32)
-    for b in range(blocks):
-        rows_of = back_in[b]
-        for e in range(local):
-            route_total = route_total + jnp.where(ids == b * local + e, rows_of[e : e + 1, :], 0.0)
-    own_route_ref[...] = route_total.astype(jnp.bfloat16)
 
     for line in range(lines):
         for half in range(2):

time: 80.5 us -> 79.7 us (0.990)
    pallas_call x1, Pallas kernels: 77.4 us -> 76.6 us  [body(): pl.pallas_call(functools.partial(kernel, lines, rows, sections), out_shap...]
where the time goes in v4:
time: 79.7 us; the launch traced here: 79.5 us
  Pallas kernels  78.9 us (99%)
    pallas_call x1, Pallas kernels, body(): pl.pallas_call(functools.partial(kernel, lines, rows, sections), out_shap...  76.6 us
    pallas_call x1, Pallas kernels, body(): pl.pallas_call(finish, out_shape=tuple((jax.ShapeDtypeStruct(shape, bf16)...  2.32 us

profile of v4, /device:TPU:1, one launch (start us, length us, event | category | flops | bytes accessed | tf_op | source)
XLA Modules:
  0.0 79.5 jit_solution(6229927363620873525)
XLA Ops:
  0.6 76.6 %shard_map.110 = (bf16[128,1024]{1,0:T(8,128)(2,1)S(1)}, bf16[8,128]{1,0:T(8,128)(2,1)S(1)}, bf16[2,1024,384]{2,1,0:T(8,128)(2,1)S(1)}, bf16[2,1024,384]{2,1,0:T(8,128)(2,1)S(1)}, bf16[2,384,1024]{2,1,0:T(8,128)(2,1)S(1)}) custom-call(s32[8,128]{1,0:T(8,128)} %bitcast.23, s32[8,128]{1,0:T(8,128)} %bitcast.24, bf16[128,1024]{1,0:T(8,128)(2,1)} %bitcast.21, ...), custom_call_target="tpu_custom_call" | custom-call | tf_op jit(solution)/shard_map/pallas_call | solution.py:438
  77.2 2.3 %shard_map.111 = (bf16[128,1024]{1,0:T(8,128)(2,1)}, bf16[8,128]{1,0:T(8,128)(2,1)}, bf16[2,1024,384]{2,1,0:T(8,128)(2,1)}, bf16[2,1024,384]{2,1,0:T(8,128)(2,1)}, bf16[2,384,1024]{2,1,0:T(8,128)(2,1)}) custom-call(bf16[128,1024]{1,0:T(8,128)(2,1)S(1)} %get-tuple-element.15.refs_0_, bf16[8,128]{1,0:T(8,128)(2,1)S(1)} %get-tuple-element.16.refs_1_, ...), custom_call_target="tpu_custom_call" | custom-call | tf_op jit(solution)/shard_map/pallas_call | solution.py:482

commit v5 on v4

--- a/solution.py
+++ b/solution.py
@@ -9,7 +9,7 @@
 from jax.sharding import PartitionSpec as P
 
 MESH = pl.DeviceIdType.MESH
-COLUMN = ((1,), (1,))
+COLUMN = ((1,), (1,), (1,), (1,))
 CUTS = len(COLUMN)
 
 
@@ -217,26 +217,30 @@
             grads[block], w_down[...], last_dims, preferred_element_type=jnp.float32
         )
         block_routes = routes[block]
-        route_rows = jnp.zeros(back_out.shape[1:], jnp.float32)
+        rest = []
         for e in range(local):
             route = jnp.sum(jnp.where(expert_row == first + e, block_routes, 0.0), axis=0, keepdims=True)
             route = jnp.sum(jnp.where(diagonal, route, 0.0), axis=1, keepdims=True)
             silu, active, slope = forward_parts[e]
             back = back_all[:, e * hidden : (e + 1) * hidden]
-            route_grad = jnp.sum(active * back, axis=1, keepdims=True)
-            route_grad = jnp.sum(jnp.where(diagonal, route_grad, 0.0), axis=0, keepdims=True)
-            route_rows = route_rows + jnp.where(back_row == e, route_grad, 0.0)
+            rest.append((route, active, back))
             back = back * route
-            hidden_grads[block, :, pl.ds(2 * e * hidden, hidden)] = (
-                back * slope
-            ).astype(jnp.bfloat16)
+            hidden_grads[block, :, pl.ds(2 * e * hidden, hidden)] = (back * slope).astype(jnp.bfloat16)
             hidden_grads[block, :, pl.ds((2 * e + 1) * hidden, hidden)] = (back * silu).astype(jnp.bfloat16)
-            scaled_all[block, :, pl.ds(e * hidden, hidden)] = (active * route).astype(jnp.bfloat16)
         total = lax.dot_general(
             hidden_grads[block], w_in[...], last_dims, preferred_element_type=jnp.float32
         )
-        back_out[block] = route_rows
-        return total.astype(jnp.bfloat16)
+
+        def finish_block():
+            route_rows = jnp.zeros(back_out.shape[1:], jnp.float32)
+            for e, (route, active, back) in enumerate(rest):
+                route_grad = jnp.sum(active * back, axis=1, keepdims=True)
+                route_grad = jnp.sum(jnp.where(diagonal, route_grad, 0.0), axis=0, keepdims=True)
+                route_rows = route_rows + jnp.where(back_row == e, route_grad, 0.0)
+                scaled_all[block, :, pl.ds(e * hidden, hidden)] = (active * route).astype(jnp.bfloat16)
+            back_out[block] = route_rows
+
+        return total.astype(jnp.bfloat16), finish_block
 
     def step(j, carry):
         after_first = j - 1
@@ -277,27 +281,29 @@
                 device_id={"expert": at(z, 1)}, device_id_type=MESH,
             ).wait_recv()
 
-        total = compute(block, wait_grads)
+        total, finish_block = compute(block, wait_grads)
+
+        @pl.when(dx == 0)
+        def _():
+            col_out[line] = total
+
+            @pl.when(j >= last_forward)
+            def _():
+                start_col(line)
+
+        @pl.when(dx > 0)
+        def _():
+            side_out[line, dx - 1] = total
+
+            @pl.when(j >= last_forward)
+            def _():
+                start_side(line, dx)
+
+        finish_block()
 
         @pl.when(j > 0)
         def _():
             back_copy(block).start()
-
-        @pl.when(dx == 0)
-        def _():
-            col_out[line] = total
-
-            @pl.when(j >= last_forward)
-            def _():
-                start_col(line)
-
-        @pl.when(dx > 0)
-        def _():
-            side_out[line, dx - 1] = total
-
-            @pl.when(j >= last_forward)
-            def _():
-                start_side(line, dx)
 
         return carry
 

time: 79.7 us -> 79.5 us (level)
  no operation moved by 1% of the time
where the time goes in v5:
time: 79.5 us; the launch traced here: 79.3 us
  Pallas kernels  78.7 us (99%)
    pallas_call x1, Pallas kernels, body(): pl.pallas_call(functools.partial(kernel, lines, rows, sections), out_shap...  76.4 us
    pallas_call x1, Pallas kernels, body(): pl.pallas_call(finish, out_shape=tuple((jax.ShapeDtypeStruct(shape, bf16)...  2.32 us

profile of v5, /device:TPU:1, one launch (start us, length us, event | category | flops | bytes accessed | tf_op | source)
XLA Modules:
  0.0 79.3 jit_solution(7452982656820273369)
XLA Ops:
  0.6 76.4 %shard_map.110 = (bf16[128,1024]{1,0:T(8,128)(2,1)S(1)}, bf16[8,128]{1,0:T(8,128)(2,1)S(1)}, bf16[2,1024,384]{2,1,0:T(8,128)(2,1)S(1)}, bf16[2,1024,384]{2,1,0:T(8,128)(2,1)S(1)}, bf16[2,384,1024]{2,1,0:T(8,128)(2,1)S(1)}) custom-call(s32[8,128]{1,0:T(8,128)} %bitcast.23, s32[8,128]{1,0:T(8,128)} %bitcast.24, bf16[128,1024]{1,0:T(8,128)(2,1)} %bitcast.21, ...), custom_call_target="tpu_custom_call" | custom-call | tf_op jit(solution)/shard_map/pallas_call | solution.py:444
  77.0 2.3 %shard_map.111 = (bf16[128,1024]{1,0:T(8,128)(2,1)}, bf16[8,128]{1,0:T(8,128)(2,1)}, bf16[2,1024,384]{2,1,0:T(8,128)(2,1)}, bf16[2,1024,384]{2,1,0:T(8,128)(2,1)}, bf16[2,384,1024]{2,1,0:T(8,128)(2,1)}) custom-call(bf16[128,1024]{1,0:T(8,128)(2,1)S(1)} %get-tuple-element.15.refs_0_, bf16[8,128]{1,0:T(8,128)(2,1)S(1)} %get-tuple-element.16.refs_1_, ...), custom_call_target="tpu_custom_call" | custom-call | tf_op jit(solution)/shard_map/pallas_call | solution.py:488
